TPU v7x, 32 devices: a whole 2x2x4 slice. The times are simulated.
32 devices in a mesh: dp: 4 (over y, x), vocab: 8 (over z, core).
Axes of the slice: x: 2, y: 2, z: 4, core: 2. Of those that a mesh axis runs over, the one named last changes fastest.
Arguments:
- hidden: bfloat16 [256, 3072], P(('dp', 'vocab')), parts along dimension 0, may hold values from -60 to 60
- weight: bfloat16 [3072, 8192], P(None, 'vocab'), may hold values from -0.32421875 to 0.32421875
- targets: int32 [256], P('dp'), parts along dimension 0, may hold values from 0 to 8191
Outputs:
- loss: float32 [4], P('dp'), parts along dimension 0
- d_hidden: bfloat16 [256, 3072], P(('dp', 'vocab')), parts along dimension 0
- d_weight: bfloat16 [12288, 8192], P('dp', 'vocab'), parts along dimension 0
There are 4 independent parts, one for each index of `dp`. A program takes and returns all parts, laid end to end along the dimension named above; an argument that names none is the same for every part. Nothing has to cross between parts.
All inputs are finite; a program needn't handle non-finite values.
Results may differ from a plain program's by a relative error of at most 0.0035.
Values may be sent and summed in bfloat16 or wider, within the bound.
A program may use at most 64 MiB of HBM per device.

v0:
```python
import jax
import jax.numpy as jnp
from jax import lax
from jax.sharding import PartitionSpec as P


def joined(value, axis, combine):
    everything = jax.tree.map(lambda part: lax.all_gather(part, axis), value)
    initial = jax.tree.map(lambda part: part[0], everything)

    def hop(k, so_far):
        return combine(so_far, jax.tree.map(lambda part: part[k], everything))

    return lax.fori_loop(1, lax.axis_size(axis), hop, initial)


def combine_stats(first, second):
    top = jnp.maximum(first[0], second[0])
    total = first[1] * jnp.exp(first[0] - top) + second[1] * jnp.exp(second[0] - top)
    return (top, total, first[2] + second[2])


def body(hidden, weight, targets):
    gathered = lax.all_gather(hidden, "vocab", axis=0, tiled=True)
    logits = jnp.dot(gathered, weight, preferred_element_type=jnp.float32)
    width = weight.shape[1]
    offset = lax.axis_index("vocab") * width
    columns = offset + lax.broadcasted_iota(jnp.int32, (1, width), 1)
    hits = columns == targets[:, None]
    picked_local = jnp.sum(jnp.where(hits, logits, jnp.zeros_like(logits)), axis=1)
    local_top = jnp.max(logits, axis=1)
    local_total = jnp.sum(jnp.exp(logits - local_top[:, None]), axis=1)
    top, total, picked = joined((local_top, local_total, picked_local), "vocab", combine_stats)
    loss = jnp.mean(top + jnp.log(total) - picked).reshape(1)
    grad_logits = (
        jnp.exp(logits - top[:, None]) / total[:, None] - hits.astype(jnp.float32)
    ).astype(jnp.bfloat16)
    d_weight = lax.dot_general(
        gathered, grad_logits, (((0,), (0,)), ((), ())), preferred_element_type=jnp.float32
    ).astype(jnp.bfloat16)
    own_rows = hidden.shape[0]
    partial_value = lax.dot_general(
        grad_logits, weight, (((1,), (1,)), ((), ())), preferred_element_type=jnp.float32
    )
    everything = lax.psum(partial_value, "vocab")
    summed = lax.dynamic_slice_in_dim(everything, lax.axis_index("vocab") * own_rows, own_rows, 0)
    return (loss, summed.astype(jnp.bfloat16), d_weight)


def solution(mesh):
    placed = (P(("dp", "vocab"), None), P(None, "vocab"), P("dp"))
    return jax.shard_map(
        body,
        mesh=mesh,
        in_specs=placed,
        out_specs=(P("dp"), P(("dp", "vocab"), None), P("dp", "vocab")),
        check_vma=False,
    )
```

profile of v0, /device:TPU:0, one launch (start us, length us, event | category | flops | bytes accessed | tf_op | source)
XLA Modules:
  0.0 96.6 jit_solution(8625070616558614490)
XLA Ops:
  0.6 0.0 copy-start
  0.6 1.2 %dynamic-slice = u32[1]{0:T(128)} dynamic-slice(u32[32]{0:T(128)} %constant.59, u32[]{:T(128)S(6)} %add.78), dynamic_slice_sizes={1} | dynamic-slice | bytes 12
  2.6 16.4 %all_gather.21 = bf16[64,3072]{1,0:T(8,128)(2,1)S(1)} all-gather(bf16[8,3072]{1,0:T(8,128)(2,1)} %param.5), channel_id=1, replica_groups=mesh['dp'=4,'vocab'=8] {'vocab'}, dimensions={0}, use_global_device_ids=true | all-gather | bytes 442368 | tf_op jit(solution)/shard_map/all_gather | solution.py:24
  19.0 4.1 %fusion.14 = (f32[64]{0:T(128)S(1)}, f32[64,1024]{1,0:T(8,128)S(1)}) fusion(bf16[64,3072]{1,0:T(8,128)(2,1)S(1)} %all_gather.21, bf16[3072,1024]{1,0:T(8,128)(2,1)} %param.6), kind=kOutput, calls=%fused_computation.21 | convolution fusion | flops 402718656 | bytes 6947072 | tf_op jit(solution)/shard_map/dot_general | solution.py:25
  23.1 0.2 dynamic-update-slice
  23.4 0.0 copy-done
  23.4 0.2 fusion.7
  23.6 0.2 dynamic-update-slice.2
  23.8 0.2 dynamic-update-slice.1
  24.0 17.2 %all-reduce.3 = (f32[512]{0:T(512)S(1)}, f32[512]{0:T(512)S(1)}, f32[512]{0:T(512)S(1)}) all-reduce(f32[512]{0:T(512)S(1)} %dynamic-update-slice, f32[512]{0:T(512)S(1)} %dynamic-update-slice.1, f32[512]{0:T(512)S(1)} %dynamic-update-slice.2), channel_id=2, replica_groups=mesh['dp'=4,'vocab'=8] {'vocab'}, use_global_device_ids=true, to_apply=%add | all-reduce | flops 1536 | bytes 12288
  41.2 0.1 reshape.21
  41.3 0.1 reshape.20
  41.4 0.1 reshape.19
  41.5 0.3 while.19
  41.8 0.6 subtract_reduce_fusion
  43.0 4.8 %fusion.11 = f32[64,3072]{1,0:T(8,128)S(1)} fusion(bf16[3072,1024]{1,0:T(8,128)(2,1)} %param.6, f32[64,1024]{1,0:T(8,128)S(1)} %get-tuple-element.210, f32[64]{0:T(128)S(1)} %get-tuple-element.182, f32[64]{0:T(128)S(1)} %get-tuple-element.181, s32[1024]{0:T(1024)S(1)} %iota_add_fusion, s32[64]{0:T(128)S(1)} %copy-done), kind=kOutput, calls=%fused_computation.20 | convolution fusion | flops 403046400 | bytes 7344896 | tf_op jit(solution)/shard_map/dot_general | solution.py:42
  47.9 33.8 %all-reduce.5 = bf16[64,3072]{1,0:T(8,128)(2,1)S(1)} all-reduce(f32[64,3072]{1,0:T(8,128)S(1)} %fusion.11), channel_id=1, replica_groups=mesh['dp'=4,'vocab'=8] {'vocab'}, use_global_device_ids=true, to_apply=%region_6.7 | all-reduce | flops 196608 | bytes 1179648 | tf_op jit(solution)/shard_map/psum | solution.py:45
  81.7 0.6 dynamic-slice_convert_fusion
  82.3 4.6 %convert_bitcast_fusion = bf16[3072,1024]{0,1:T(8,128)(2,1)} fusion(bf16[64,3072]{1,0:T(8,128)(2,1)S(1)} %all_gather.21, f32[64,1024]{1,0:T(8,128)S(1)} %get-tuple-element.210, f32[64]{0:T(128)S(1)} %get-tuple-element.182, f32[64]{0:T(128)S(1)} %get-tuple-element.181, s32[1024]{0:T(1024)S(1)} %iota_add_fusion, s32[64]{0:T(128)S(1)} %copy-done), kind=kOutput, calls=%fused_computation.10 | convolution fusion | flops 406192128 | bytes 6951680 | tf_op jit(solution)/shard_map/dot_general | solution.py:38
  86.9 8.6 %copy.6 = bf16[3072,1024]{1,0:T(8,128)(2,1)} copy(bf16[3072,1024]{0,1:T(8,128)(2,1)} %convert_bitcast_fusion) | data formatting | bytes 12582912
  (14 shorter events, 0.2 us)
Async XLA Ops:
  0.6 22.7 %copy-start = (s32[64]{0:T(128)S(1)}, s32[64]{0:T(128)}, u32[]{:S(2)}) copy-start(s32[64]{0:T(128)} %param.7) | copy-start | bytes 772
where the time goes:
time: 97.1 us; the launch traced here: 96.6 us
  blocking collectives  67.4 us (69%)
  matrix products  13.5 us (14%)
  local copies, waits for them, and re-layouts  11.4 us (12%)
  between operations  3.16 us (3%)
  other arithmetic  1.03 us (1%)
    psum x1, blocking collectives, body(): everything = lax.psum(partial_value, 'vocab')  33.8 us
    unnamed x1, blocking collectives  17.2 us
    all_gather x1, blocking collectives, body(): gathered = lax.all_gather(hidden, 'vocab', axis=0, tiled=True)  16.4 us
    unnamed x10, local copies, waits for them, and re-layouts  10.6 us
    dot_general x1, matrix products, body(): lax.dot_general(grad_logits, weight, (((1,), (1,)), ((), ())), preferred_...  4.85 us
    dot_general x1, matrix products, body(): lax.dot_general(gathered, grad_logits, (((0,), (0,)), ((), ())), preferre...  4.58 us
    dot_general x1, matrix products, body(): logits = jnp.dot(gathered, weight, preferred_element_type=jnp.float32)  4.09 us

commit v1 on v0

--- a/solution.py
+++ b/solution.py
@@ -42,7 +42,16 @@
     partial_value = lax.dot_general(
         grad_logits, weight, (((1,), (1,)), ((), ())), preferred_element_type=jnp.float32
     )
-    everything = lax.psum(partial_value, "vocab")
+
+    def _scan_tails(values, peer_axis):
+        count_all = lax.axis_size(peer_axis)
+        part_next = lambda carry_out: [(no, no ^ carry_out) for no in range(count_all)]
+        formed = values
+        for i0 in range(count_all.bit_length() - 1):
+            formed = formed + lax.ppermute(formed, peer_axis, part_next(1 << i0))
+        return formed
+
+    everything = _scan_tails(partial_value, "vocab")
     summed = lax.dynamic_slice_in_dim(everything, lax.axis_index("vocab") * own_rows, own_rows, 0)
     return (loss, summed.astype(jnp.bfloat16), d_weight)
 

time: 97.1 us -> 108 us (1.11)
  waiting for transfers between devices: 0 us -> 43.9 us
  blocking collectives: 67.4 us -> 33.6 us
    ppermute x0 -> x3, waiting for transfers between devices: none -> 43.9 us  [_scan_tails(): formed = formed + lax.ppermute(formed, peer_axis, part_next(1 << i0))]
    psum x1 -> x0, blocking collectives: 33.8 us -> none  [body(): everything = lax.psum(partial_value, 'vocab')]
  transfers between devices with their start and end apart: 0 -> 3, of which waited for: 0 -> 3; matrix products, arithmetic and copies ran while one was open for 0% -> 13% of each run, Pallas kernels for 0% -> 0%
where the time goes in v1:
time: 108 us; the launch traced here: 107 us
  waiting for transfers between devices  43.9 us (41%)
  blocking collectives  33.6 us (31%)
  matrix products  13.5 us (12%)
  local copies, waits for them, and re-layouts  10.8 us (10%)
  between operations  3.17 us (3%)
  other arithmetic  1.86 us (2%)
    ppermute x3, waiting for transfers between devices, _scan_tails(): formed = formed + lax.ppermute(formed, peer_axis, part_next(1 << i0))  43.9 us
    unnamed x1, blocking collectives  17.2 us
    all_gather x1, blocking collectives, body(): gathered = lax.all_gather(hidden, 'vocab', axis=0, tiled=True)  16.4 us
    unnamed x10, local copies, waits for them, and re-layouts  10.5 us
    dot_general x1, matrix products, body(): lax.dot_general(grad_logits, weight, (((1,), (1,)), ((), ())), preferred_...  4.85 us
    dot_general x1, matrix products, body(): lax.dot_general(gathered, grad_logits, (((0,), (0,)), ((), ())), preferre...  4.58 us
    dot_general x1, matrix products, body(): logits = jnp.dot(gathered, weight, preferred_element_type=jnp.float32)  4.09 us
  transfers between devices with their start and end apart: 3, of which 3 were waited for; matrix products, arithmetic and copies ran while one was open for 13% of the time, Pallas kernels for 0%

profile of v1, /device:TPU:0, one launch (start us, length us, event | category | flops | bytes accessed | tf_op | source)
XLA Modules:
  0.0 107.1 jit_solution(15808542395336371869)
XLA Ops:
  0.6 0.0 copy-start
  0.7 16.4 %all_gather.21 = bf16[64,3072]{1,0:T(8,128)(2,1)S(1)} all-gather(bf16[8,3072]{1,0:T(8,128)(2,1)} %param.5), channel_id=1, replica_groups=mesh['dp'=4,'vocab'=8] {'vocab'}, dimensions={0}, use_global_device_ids=true | all-gather | bytes 442368 | tf_op jit(solution)/shard_map/all_gather | solution.py:24
  17.1 1.2 %dynamic-slice = u32[1]{0:T(128)} dynamic-slice(u32[32]{0:T(128)} %constant.59, u32[]{:T(128)S(6)} %add.88), dynamic_slice_sizes={1} | dynamic-slice | bytes 12
  19.0 4.1 %fusion.15 = (f32[64]{0:T(128)S(1)}, f32[64,1024]{1,0:T(8,128)S(1)}) fusion(bf16[64,3072]{1,0:T(8,128)(2,1)S(1)} %all_gather.21, bf16[3072,1024]{1,0:T(8,128)(2,1)} %param.6), kind=kOutput, calls=%fused_computation.22 | convolution fusion | flops 402718656 | bytes 6947072 | tf_op jit(solution)/shard_map/dot_general | solution.py:25
  23.1 0.2 dynamic-update-slice
  23.3 0.0 copy-done
  23.3 0.2 fusion.7
  23.6 0.2 dynamic-update-slice.2
  23.8 0.2 dynamic-update-slice.1
  24.0 17.2 %all-reduce.3 = (f32[512]{0:T(512)S(1)}, f32[512]{0:T(512)S(1)}, f32[512]{0:T(512)S(1)}) all-reduce(f32[512]{0:T(512)S(1)} %dynamic-update-slice, f32[512]{0:T(512)S(1)} %dynamic-update-slice.1, f32[512]{0:T(512)S(1)} %dynamic-update-slice.2), channel_id=2, replica_groups=mesh['dp'=4,'vocab'=8] {'vocab'}, use_global_device_ids=true, to_apply=%add | all-reduce | flops 1536 | bytes 12288
  41.2 0.1 reshape.21
  41.3 0.1 reshape.20
  41.4 0.1 reshape.19
  41.4 0.3 while.19
  41.7 4.8 %fusion.12 = f32[64,3072]{1,0:T(8,128)S(1)} fusion(bf16[3072,1024]{1,0:T(8,128)(2,1)} %param.6, f32[64,1024]{1,0:T(8,128)S(1)} %get-tuple-element.210, f32[64]{0:T(128)S(1)} %get-tuple-element.182, f32[64]{0:T(128)S(1)} %get-tuple-element.181, s32[1024]{0:T(1024)S(1)} %iota_add_fusion, s32[64]{0:T(128)S(1)} %copy-done), kind=kOutput, calls=%fused_computation.21 | convolution fusion | flops 403046400 | bytes 7344896 | tf_op jit(solution)/shard_map/dot_general | solution.py:42
  46.6 0.1 collective-permute-start
  46.7 2.3 %collective-permute-done = f32[64,3072]{1,0:T(8,128)S(1)} collective-permute-done((f32[64,3072]{1,0:T(8,128)S(1)}, f32[64,3072]{1,0:T(8,128)S(1)}, u32[]{:S(2)}, u32[]{:S(2)}) %collective-permute-start) | collective-permute-done | bytes 786464 | tf_op jit(solution)/shard_map/ppermute | solution.py:51
  48.9 0.1 add.84
  49.1 0.1 collective-permute-start.1
  49.1 19.6 %collective-permute-done.1 = f32[64,3072]{1,0:T(8,128)S(1)} collective-permute-done((f32[64,3072]{1,0:T(8,128)S(1)}, f32[64,3072]{1,0:T(8,128)S(1)}, u32[]{:S(2)}, u32[]{:S(2)}) %collective-permute-start.1) | collective-permute-done | bytes 786464 | tf_op jit(solution)/shard_map/ppermute | solution.py:51
  68.7 0.1 add.85
  68.8 0.1 collective-permute-start.2
  68.9 4.6 %convert_bitcast_fusion = bf16[3072,1024]{0,1:T(8,128)(2,1)} fusion(bf16[64,3072]{1,0:T(8,128)(2,1)S(1)} %all_gather.21, f32[64,1024]{1,0:T(8,128)S(1)} %get-tuple-element.210, f32[64]{0:T(128)S(1)} %get-tuple-element.182, f32[64]{0:T(128)S(1)} %get-tuple-element.181, s32[1024]{0:T(1024)S(1)} %iota_add_fusion, s32[64]{0:T(128)S(1)} %copy-done), kind=kOutput, calls=%fused_computation.10 | convolution fusion | flops 406192128 | bytes 6951680 | tf_op jit(solution)/shard_map/dot_general | solution.py:38
  73.5 8.6 %copy.6 = bf16[3072,1024]{1,0:T(8,128)(2,1)} copy(bf16[3072,1024]{0,1:T(8,128)(2,1)} %convert_bitcast_fusion) | data formatting | bytes 12582912
  82.1 0.6 subtract_reduce_fusion
  83.3 22.0 %collective-permute-done.2 = f32[64,3072]{1,0:T(8,128)S(1)} collective-permute-done((f32[64,3072]{1,0:T(8,128)S(1)}, f32[64,3072]{1,0:T(8,128)S(1)}, u32[]{:S(2)}, u32[]{:S(2)}) %collective-permute-start.2) | collective-permute-done | bytes 786464 | tf_op jit(solution)/shard_map/ppermute | solution.py:51
  105.3 0.6 fusion.10
  (14 shorter events, 0.2 us)
Async XLA Ops:
  0.6 22.7 %copy-start = (s32[64]{0:T(128)S(1)}, s32[64]{0:T(128)}, u32[]{:S(2)}) copy-start(s32[64]{0:T(128)} %param.7) | copy-start | bytes 772
  46.6 2.4 %collective-permute-start = (f32[64,3072]{1,0:T(8,128)S(1)}, f32[64,3072]{1,0:T(8,128)S(1)}, u32[]{:S(2)}, u32[]{:S(2)}) collective-permute-start(f32[64,3072]{1,0:T(8,128)S(1)} %fusion.12), channel_id=1, source_target_pairs={{0,1},{1,0},{2,3},{3,2},{4,5},{5,4},{6,7},{7,6},{8,9},{9,8},{10,11... | collective-permute-start | bytes 2359304 | tf_op jit(solution)/shard_map/ppermute | solution.py:51
  49.1 19.6 %collective-permute-start.1 = (f32[64,3072]{1,0:T(8,128)S(1)}, f32[64,3072]{1,0:T(8,128)S(1)}, u32[]{:S(2)}, u32[]{:S(2)}) collective-permute-start(f32[64,3072]{1,0:T(8,128)S(1)} %add.84), channel_id=1, source_target_pairs={{0,2},{1,3},{2,0},{3,1},{4,6},{5,7},{6,4},{7,5},{8,10},{9,11},{10,... | collective-permute-start | bytes 2359304 | tf_op jit(solution)/shard_map/ppermute | solution.py:51
  68.8 36.5 %collective-permute-start.2 = (f32[64,3072]{1,0:T(8,128)S(1)}, f32[64,3072]{1,0:T(8,128)S(1)}, u32[]{:S(2)}, u32[]{:S(2)}) collective-permute-start(f32[64,3072]{1,0:T(8,128)S(1)} %add.85), channel_id=1, source_target_pairs={{0,4},{1,5},{2,6},{3,7},{4,0},{5,1},{6,2},{7,3},{8,12},{9,13},{10,... | collective-permute-start | bytes 2359304 | tf_op jit(solution)/shard_map/ppermute | solution.py:51
